TPU v7x, 32 devices: a whole 2x2x4 slice. The times are simulated.
32 devices in a mesh: seq: 16 (over z, y, core), exp: 2 (over x).
Axes of the slice: x: 2, y: 2, z: 4, core: 2. Of those that a mesh axis runs over, the one named last changes fastest.
Arguments:
- hidden_in: bfloat16 [6, 6144], P('exp', 'seq'), may hold values from -2 to 2
- queries: bfloat16 [6, 6144], P(None, 'exp'), may hold values from -40 to 40
- key_cache: bfloat16 [6, 8192, 1024], P(None, 'seq', 'exp'), may hold values from -16 to 16
- value_cache: bfloat16 [6, 8192, 1024], P(None, 'seq', 'exp'), may hold values from -6 to 6
- lengths: int32 [6], replicated, may hold values from 2 to 8192
- out_weight: bfloat16 [6144, 6144], P('exp', 'seq'), may hold values from -0.078125 to 0.078125
- norm_gain: float32 [6144], P('seq'), may hold values from 0.1 to 1.9
- router: bfloat16 [6144, 8], P('seq'), may hold values from -0.078125 to 0.078125
- expert_ids: int32 [6, 2], P('exp'), may hold values from 0 to 7, as said below
- capacity: int32 [8], replicated, may hold values from 1 to 3, as said below
- w_gate: bfloat16 [8, 6144, 8192], P('exp', None, 'seq'), may hold values from -0.078125 to 0.078125
- w_up: bfloat16 [8, 6144, 8192], P('exp', None, 'seq'), may hold values from -0.078125 to 0.078125
- w_down: bfloat16 [8, 8192, 6144], P('exp', 'seq'), may hold values from -0.09375 to 0.09375
Outputs:
- layer_out: bfloat16 [6, 6144], P('exp', 'seq')
Inputs may be any that keep to these rules, and one draw needn't show every extreme that they name: lengths[b] counts sequence b's live cache positions, the newest token's included. `expert_ids`: the two experts of a token differ. One expert is named by every token; any other expert is named at most 3 times within one aligned block of 3 tokens. The expert that every token names has capacity 3.
All inputs are finite; a program needn't handle non-finite values.
Results may differ from a plain program's by a relative error of at most 0.0085.
Values may be sent and summed in bfloat16 or wider, within the bound.
A program may use at most 128 MiB of HBM per device.

v0:
```python
import math
import jax
import jax.numpy as jnp
from jax import lax
from jax.sharding import PartitionSpec as P

D = 6144
HEADS = 48
KV_HEADS = 8
HEAD_DIM = 128
EXPERTS = 8
masked_score = -1e30
norm_eps = 1e-05


def joined(value, axis, join):
    pieces = jax.tree.map(lambda part: lax.all_gather(part, axis), value)
    head = jax.tree.map(lambda part: part[0], pieces)
    tail = jax.tree.map(lambda part: part[1:], pieces)
    running, _ = lax.scan(lambda running, share: (join(running, share), None), head, tail)
    return running


def merge_partial_results(left_part, right_part):
    left_maximum_score, left_denom, left_sum = left_part
    right_peak, right_denom, right_sum = right_part
    joint_peak = jnp.maximum(left_maximum_score, right_peak)
    left_factor = jnp.exp(left_maximum_score - joint_peak)
    right_factor = jnp.exp(right_peak - joint_peak)
    return (
        joint_peak,
        left_denom * left_factor + right_denom * right_factor,
        left_sum * left_factor[..., None] + right_sum * right_factor[..., None],
    )


def on_device(
    hidden_in,
    queries,
    key_cache,
    value_cache,
    lengths,
    out_weight,
    norm_gain,
    router,
    expert_ids,
    capacity,
    w_gate,
    w_up,
    w_down,
):
    seq_count = queries.shape[0]
    group_size = HEADS // KV_HEADS
    kv_local = key_cache.shape[2] // HEAD_DIM
    span_local = key_cache.shape[1]
    query_heads = queries.reshape(seq_count, kv_local, group_size, HEAD_DIM)
    key_rows = key_cache.reshape(seq_count, span_local, kv_local, HEAD_DIM)
    value_rows = value_cache.reshape(seq_count, span_local, kv_local, HEAD_DIM).astype(jnp.float32)
    first_place = lax.axis_index("seq") * span_local
    places = first_place + jnp.arange(span_local, dtype=jnp.int32)
    live_mask = (places[None, :] < lengths[:, None])[:, None, None, :]
    scores = jnp.einsum(
        "bkgd,bjkd->bkgj", query_heads, key_rows, preferred_element_type=jnp.float32
    ) * (1.0 / math.sqrt(HEAD_DIM))
    scores = jnp.where(live_mask, scores, masked_score)
    local_peak = jnp.max(scores, axis=-1)
    attn_weights = jnp.where(live_mask, jnp.exp(scores - local_peak[..., None]), 0.0)
    local_sum = jnp.einsum(
        "bkgj,bjkd->bkgd", attn_weights, value_rows, precision=lax.Precision.HIGHEST
    )
    global_peak, denom_sum, weighted = joined(
        (local_peak, jnp.sum(attn_weights, axis=-1), local_sum), "seq", merge_partial_results
    )
    attended = (
        (weighted / denom_sum[..., None])
        .reshape(seq_count, kv_local * group_size * HEAD_DIM)
        .astype(jnp.bfloat16)
    )
    partial_value = jnp.dot(attended, out_weight, preferred_element_type=jnp.float32)
    projected = lax.psum_scatter(partial_value, "exp", scatter_dimension=0, tiled=True)
    residual = hidden_in.astype(jnp.float32) + projected
    gained = residual * norm_gain
    router_wide = router.astype(jnp.float32)
    squares = jnp.sum(residual * residual, axis=-1)
    total_sq = lax.psum(squares, "seq")
    scale_row = lax.rsqrt(total_sq / D + norm_eps)
    logits = lax.psum(
        jnp.dot(gained * scale_row[:, None], router_wide, precision=lax.Precision.HIGHEST), "seq"
    )
    normed = (gained * scale_row[:, None]).astype(jnp.bfloat16)
    row_total = expert_ids.shape[0]
    onehot_int = (
        expert_ids[:, :, None] == jnp.arange(EXPERTS, dtype=jnp.int32)[None, None, :]
    ).astype(jnp.int32)
    name_count = jnp.sum(onehot_int, axis=1)
    row_order = jnp.arange(row_total, dtype=jnp.int32)
    before = (row_order[None, :] < row_order[:, None]).astype(jnp.int32)
    earlier = jnp.dot(before, name_count)
    slot_rank = jnp.sum(onehot_int * earlier[:, None, :], axis=-1)
    slot_limit = jnp.sum(onehot_int * capacity[None, None, :], axis=-1)
    kept_mask = (slot_rank < slot_limit).astype(jnp.float32)
    expert_indicator = onehot_int.astype(jnp.float32)
    chosen = jnp.sum(expert_indicator * logits[:, None, :], axis=-1)
    gate_weight = jax.nn.sigmoid(chosen - chosen[:, ::-1])
    slot_match = (slot_rank[:, :, None] == row_order[None, None, :]).astype(jnp.float32)
    placing = jnp.einsum("rke,rks->esr", expert_indicator * kept_mask[:, :, None], slot_match)
    buffer = jnp.einsum(
        "esr,rd->esd", placing.astype(jnp.bfloat16), normed, preferred_element_type=jnp.float32
    ).astype(jnp.bfloat16)
    dispatched = lax.all_to_all(buffer, "exp", split_axis=0, concat_axis=1, tiled=True)
    shard_rows = lax.all_gather(dispatched, "seq", axis=2, tiled=True)
    gate_next = jnp.einsum("ern,enf->erf", shard_rows, w_gate, preferred_element_type=jnp.float32)
    up_next = jnp.einsum("ern,enf->erf", shard_rows, w_up, preferred_element_type=jnp.float32)
    hidden_act = (jax.nn.silu(gate_next) * up_next).astype(jnp.bfloat16)
    partial_out = jnp.einsum("erf,efd->erd", hidden_act, w_down, preferred_element_type=jnp.float32)
    blend_table = jnp.einsum(
        "rke,rks->esr", expert_indicator * (gate_weight * kept_mask)[:, :, None], slot_match
    )
    reduced_output = lax.psum_scatter(partial_out, "seq", scatter_dimension=2, tiled=True)
    returned = lax.all_to_all(reduced_output, "exp", split_axis=1, concat_axis=0, tiled=True)
    combined = jnp.einsum("esr,esd->rd", blend_table, returned, precision=lax.Precision.HIGHEST)
    return (residual + combined).astype(jnp.bfloat16)


def solution(mesh):
    in_specs = (
        P("exp", "seq"),
        P(None, "exp"),
        P(None, "seq", "exp"),
        P(None, "seq", "exp"),
        P(),
        P("exp", "seq"),
        P("seq"),
        P("seq", None),
        P("exp", None),
        P(),
        P("exp", None, "seq"),
        P("exp", None, "seq"),
        P("exp", "seq", None),
    )
    out_specs = P("exp", "seq")
    return jax.shard_map(
        on_device, mesh=mesh, in_specs=in_specs, out_specs=out_specs, check_vma=False
    )
```

profile of v0, /device:TPU:0, one launch (start us, length us, event | category | flops | bytes accessed | tf_op | source)
XLA Modules:
  0.0 272.3 jit_solution(8240845647066863271)
XLA Ops:
  6.5 1.6 reshape.56
  8.2 0.9 broadcast_compare_fusion
  9.1 1.8 fusion.49
  10.9 1.4 fusion.4
  12.3 0.7 copy.28
  13.1 23.7 %all-gather = f32[96,4,6]{2,1,0:T(4,128)S(1)} all-gather(f32[6,4,6]{2,1,0:T(4,128)S(1)} %get-tuple-element.74), channel_id=2, replica_groups=mesh['seq'=16,'exp'=2] {'seq'}, dimensions={0}, use_global_device_ids=true | all-gather | bytes 9792 | tf_op jit(solution)/shard_map/all_gather | solution.py:17
  36.8 0.2 fusion.20
  37.0 18.4 %all-gather.1 = f32[96,4,6]{2,1,0:T(4,128)S(1)} all-gather(f32[6,4,6]{2,1,0:T(4,128)S(1)} %fusion.20), channel_id=3, replica_groups=mesh['seq'=16,'exp'=2] {'seq'}, dimensions={0}, use_global_device_ids=true | all-gather | bytes 9792 | tf_op jit(solution)/shard_map/all_gather | solution.py:17
  55.5 0.7 dynamic-slice
  57.0 0.9 slice.32
  57.9 2.3 slice.35
  60.3 16.4 %while.14 = (s32[]{:T(128)}, f32[6,4,6]{2,1,0:T(4,128)S(1)}, f32[6,4,6]{2,1,0:T(4,128)S(1)}, f32[6,4,6,128]{3,2,1,0:T(8,128)S(1)}, f32[15,6,4,6]{3,2,1,0:T(4,128...) while((s32[]{:T(128)}, f32[6,4,6]{2,1,0:T(4,128)S(1)}, ...), condition=%wide.region_3.4_spmd, body=%wide.region_2.3_spmd.sunk | while | flops 56162 | bytes 374501 | solution.py:20
  60.3 0.9 constant_dynamic-slice_fusion.2
  61.2 0.1 fusion.70
  61.4 0.9 constant_dynamic-slice_fusion.2
  62.3 0.1 fusion.70
  62.5 0.9 constant_dynamic-slice_fusion.2
  63.4 0.1 fusion.70
  63.6 0.9 constant_dynamic-slice_fusion.2
  64.5 0.1 fusion.70
  64.7 0.9 constant_dynamic-slice_fusion.2
  65.6 0.1 fusion.70
  65.8 0.9 constant_dynamic-slice_fusion.2
  66.7 0.1 fusion.70
  66.9 0.9 constant_dynamic-slice_fusion.2
  67.7 0.1 fusion.70
  67.9 0.9 constant_dynamic-slice_fusion.2
  68.8 0.1 fusion.70
  69.0 0.9 constant_dynamic-slice_fusion.2
  69.9 0.1 fusion.70
  70.1 0.9 constant_dynamic-slice_fusion.2
  71.0 0.1 fusion.70
  71.2 0.9 constant_dynamic-slice_fusion.2
  72.1 0.1 fusion.70
  72.3 0.9 constant_dynamic-slice_fusion.2
  73.2 0.1 fusion.70
  73.4 0.9 constant_dynamic-slice_fusion.2
  74.3 0.1 fusion.70
  74.5 0.9 constant_dynamic-slice_fusion.2
  75.4 0.1 fusion.70
  75.6 0.9 constant_dynamic-slice_fusion.2
  76.5 0.1 fusion.70
  76.8 0.4 fusion.50
  77.2 8.1 %all-reduce = f32[6,384]{1,0:T(8,128)S(1)} all-reduce(f32[6,384]{1,0:T(8,128)S(1)} %fusion.50), channel_id=5, replica_groups=mesh['seq'=16,'exp'=2] {'exp'}, use_global_device_ids=true, to_apply=%region_4.5.clone | all-reduce | flops 2304 | bytes 18432
  85.3 0.1 multiply_reduce_fusion
  85.4 0.1 fusion.40
  85.5 29.5 %psum.14 = f32[3]{0:T(128)S(1)} all-reduce(f32[3]{0:T(128)S(1)} %multiply_reduce_fusion), channel_id=1, replica_groups=mesh['seq'=16,'exp'=2] {'seq'}, use_global_device_ids=true, to_apply=%region_9.10 | all-reduce | flops 3 | bytes 24 | tf_op jit(solution)/shard_map/psum | solution.py:85
  115.0 0.2 fusion.26
  115.2 0.3 select_reduce_fusion
  115.5 29.5 %psum.15 = f32[3,8]{1,0:T(4,128)S(1)} all-reduce(f32[3,8]{1,0:T(4,128)S(1)} %fusion.26), channel_id=1, replica_groups=mesh['seq'=16,'exp'=2] {'seq'}, use_global_device_ids=true, to_apply=%region_10.11 | all-reduce | flops 24 | bytes 192 | tf_op jit(solution)/shard_map/psum | solution.py:87
  145.0 0.2 fusion.30
  145.2 0.3 fusion.19
  145.5 0.2 convolution_convert_fusion
  145.7 6.3 %all_to_all.36 = bf16[8,3,384]{2,1,0:T(4,128)(2,1)S(1)} all-to-all(bf16[8,3,384]{2,1,0:T(4,128)(2,1)S(1)} %copy.33), channel_id=1, replica_groups=mesh['seq'=16,'exp'=2] {'exp'}, dimensions={0} | all-to-all | bytes 36864 | tf_op jit(solution)/shard_map/all_to_all | solution.py:110
  152.0 18.3 %all_gather.27 = bf16[4,6,6144]{2,1,0:T(8,128)(2,1)S(1)} all-gather(bf16[4,6,384]{2,1,0:T(8,128)(2,1)S(1)} %copy.35), channel_id=1, replica_groups=mesh['seq'=16,'exp'=2] {'seq'}, dimensions={2}, use_global_device_ids=true | all-gather | bytes 313344 | tf_op jit(solution)/shard_map/all_gather | solution.py:111
  170.3 9.9 %fusion.51 = f32[4,6,512]{2,1,0:T(8,128)S(1)} fusion(bf16[4,6,6144]{2,1,0:T(8,128)(2,1)S(1)} %all_gather.27, bf16[4,6144,512]{2,1,0:T(8,128)(2,1)} %param.25), kind=kOutput, calls=%fused_computation.70 | convolution fusion | flops 150994944 | bytes 25509888 | tf_op jit(solution)/shard_map/ern,enf->erf/dot_general | solution.py:112
  180.2 9.9 %fusion.16 = bf16[4,6,512]{2,1,0:T(8,128)(2,1)S(1)} fusion(bf16[4,6,6144]{2,1,0:T(8,128)(2,1)S(1)} %all_gather.27, bf16[4,6144,512]{2,1,0:T(8,128)(2,1)} %param.26, f32[4,6,512]{2,1,0:T(8,128)S(1)} %fusion.51), kind=kOutput, calls=%fused_computation.19 | convolution fusion | flops 151068672 | bytes 25534464 | tf_op jit(solution)/shard_map/ern,enf->erf/dot_general | solution.py:113
  190.1 10.9 %fusion.52 = f32[4,6,6144]{2,1,0:T(8,128)} fusion(bf16[4,6,512]{2,1,0:T(8,128)(2,1)S(1)} %fusion.16, bf16[4,512,6144]{2,1,0:T(8,128)(2,1)} %param.27), kind=kOutput, calls=%fused_computation.71 | convolution fusion | flops 150994944 | bytes 25780224 | tf_op jit(solution)/shard_map/erf,efd->erd/dot_general | solution.py:115
  201.1 54.9 %reduce-scatter.2.cloned.1.call-done = f32[4,6,384]{2,1,0:T(8,128)} async-done(((f32[4,6,6144]{2,1,0:T(8,128)}), f32[4,6,384]{2,1,0:T(8,128)}) %reduce-scatter.2.cloned.1.call-update) | async-done | bytes 36880 | tf_op jit(solution)/shard_map/reduce_scatter | solution.py:119
  255.9 1.4 copy.36
  257.4 3.3 %all-to-all-start.1 = ((f32[4,6,384]{2,0,1:T(4,128)}), f32[4,6,384]{2,0,1:T(4,128)S(1)}, u32[]{:S(2)}, u32[]{:S(2)}) async-start(f32[4,6,384]{2,0,1:T(4,128)} %copy.36), calls=%async_computation.2 | async-start | bytes 73728 | tf_op jit(solution)/shard_map/all_to_all | solution.py:120
  260.6 0.3 convolution_bitcast_fusion.1
  260.9 3.7 %all-to-all-done.1 = f32[4,6,384]{2,0,1:T(4,128)S(1)} async-done(((f32[4,6,384]{2,0,1:T(4,128)}), f32[4,6,384]{2,0,1:T(4,128)S(1)}, u32[]{:S(2)}, u32[]{:S(2)}) %all-to-all-start.1) | async-done | bytes 36896 | tf_op jit(solution)/shard_map/all_to_all | solution.py:120
  264.6 0.8 fusion.18
  (59 shorter events, 1.2 us)
Async XLA Ops:
  6.5 2.5 copy-start
  6.5 50.4 %all-gather.5.cloned.1.call-start = ((), (), s32[]{:S(2)}) async-start(), calls=%async_computation.4 | async-start | bytes 1253376 | tf_op jit(solution)/shard_map/all_gather | solution.py:17
  8.2 2.7 %copy-start.2 = (bf16[6,512,512]{2,1,0:T(8,128)(2,1)S(1)}, bf16[6,512,512]{2,1,0:T(8,128)(2,1)}, u32[]{:S(2)}) copy-start(bf16[6,512,512]{2,1,0:T(8,128)(2,1)} %param.18) | copy-start | bytes 9437188
  10.9 44.5 %copy-start.5 = (s32[3,2]{0,1:T(2,128)S(1)}, s32[3,2]{0,1:T(2,128)}, u32[]{:S(2)}) copy-start(s32[3,2]{0,1:T(2,128)} %param.23) | copy-start | bytes 76
  10.9 44.6 %copy-start.9 = (u32[32]{0:T(128)S(1)}, u32[32]{0:T(128)}, u32[]{:S(2)}) copy-start(u32[32]{0:T(128)} %constant.44) | copy-start | bytes 388
  13.0 242.9 %reduce-scatter.2.cloned.1.call-start = ((), (), s32[]{:S(2)}) async-start(), calls=%async_computation.3 | async-start | bytes 835584 | tf_op jit(solution)/shard_map/reduce_scatter | solution.py:119
  37.0 39.8 %copy-start.3 = (bf16[3072,384]{1,0:T(8,128)(2,1)S(1)}, bf16[3072,384]{1,0:T(8,128)(2,1)}, u32[]{:S(2)}) copy-start(bf16[3072,384]{1,0:T(8,128)(2,1)} %param.20) | copy-start | bytes 7077892
  60.2 25.0 %copy-start.4 = (bf16[3,384]{1,0:T(4,128)(2,1)S(1)}, bf16[3,384]{1,0:T(4,128)(2,1)}, u32[]{:S(2)}) copy-start(bf16[3,384]{1,0:T(4,128)(2,1)} %param.15) | copy-start | bytes 6916
  60.3 54.8 %copy-start.7 = (bf16[384,8]{0,1:T(8,128)(2,1)S(1)}, bf16[384,8]{0,1:T(8,128)(2,1)}, u32[]{:S(2)}) copy-start(bf16[384,8]{0,1:T(8,128)(2,1)} %param.22) | copy-start | bytes 18436
  60.3 54.8 %copy-start.8 = (f32[384]{0:T(512)S(1)}, f32[384]{0:T(512)}, u32[]{:S(2)}) copy-start(f32[384]{0:T(512)} %param.21) | copy-start | bytes 4612
  60.3 55.0 %copy-start.6 = (s32[8]{0:T(128)S(1)}, s32[8]{0:T(128)}, u32[]{:S(2)}) copy-start(s32[8]{0:T(128)} %param.24) | copy-start | bytes 100
  190.1 75.3 %copy-start.1 = (bf16[6,512,512]{2,1,0:T(8,128)(2,1)S(1)}, bf16[6,512,512]{2,1,0:T(8,128)(2,1)}, u32[]{:S(2)}) copy-start(bf16[6,512,512]{2,1,0:T(8,128)(2,1)} %param.17) | copy-start | bytes 9437188
  257.4 7.2 %all-to-all-start.1 = ((f32[4,6,384]{2,0,1:T(4,128)}), f32[4,6,384]{2,0,1:T(4,128)S(1)}, u32[]{:S(2)}, u32[]{:S(2)}) async-start(f32[4,6,384]{2,0,1:T(4,128)} %copy.36), calls=%async_computation.2 | async-start | bytes 73728 | tf_op jit(solution)/shard_map/all_to_all | solution.py:120
Sparse Core Ops, SparseCore 0:
  13.1 41.2 all-gather.4
  201.2 54.6 reduce-scatter.1
where the time goes:
time: 273 us; the launch traced here: 272 us
  blocking collectives  134 us (49%)
  waiting for transfers between devices  58.6 us (21%)
  matrix products  36.3 us (13%)
  local copies, waits for them, and re-layouts  21.4 us (8%)
  between operations  14.3 us (5%)
  other arithmetic  4.47 us (2%)
  starting transfers between devices  3.3 us (1%)
    reduce_scatter x1, waiting for transfers between devices, on_device(): lax.psum_scatter(partial_out, 'seq', scatter_dimension=2, tiled=True)  54.9 us
    all_gather x2, blocking collectives, joined(): pieces = jax.tree.map(lambda part: lax.all_gather(part, axis), value)  42.1 us
    psum x1, blocking collectives, on_device(): lax.psum(jnp.dot(gained * scale_row[:, None], router_wide, precision=lax....  29.5 us
    psum x1, blocking collectives, on_device(): total_sq = lax.psum(squares, 'seq')  29.5 us
    all_gather x1, blocking collectives, on_device(): shard_rows = lax.all_gather(dispatched, 'seq', axis=2, tiled=True)  18.3 us
    dynamic_slice x15, local copies, waits for them, and re-layouts, joined(): lax.scan(lambda running, share: (join(running, share), None), head, tail)  13.4 us
    dot_general x1, matrix products, on_device(): jnp.einsum('erf,efd->erd', hidden_act, w_down, preferred_element_type=jnp...  10.9 us
    dot_general x1, matrix products, on_device(): jnp.einsum('ern,enf->erf', shard_rows, w_up, preferred_element_type=jnp.f...  9.94 us
  transfers between devices with their start and end apart: 3, of which 2 were waited for; matrix products, arithmetic and copies ran while one was open for 1% of the time, Pallas kernels for 0%

commit v1 on v0

--- a/solution.py
+++ b/solution.py
@@ -84,8 +84,12 @@
     squares = jnp.sum(residual * residual, axis=-1)
     total_sq = lax.psum(squares, "seq")
     scale_row = lax.rsqrt(total_sq / D + norm_eps)
-    logits = lax.psum(
-        jnp.dot(gained * scale_row[:, None], router_wide, precision=lax.Precision.HIGHEST), "seq"
+    logits = jnp.sum(
+        lax.all_gather(
+            jnp.dot(gained * scale_row[:, None], router_wide, precision=lax.Precision.HIGHEST),
+            "seq",
+        ),
+        axis=0,
     )
     normed = (gained * scale_row[:, None]).astype(jnp.bfloat16)
     row_total = expert_ids.shape[0]

time: 273 us -> 261 us (0.956)
  blocking collectives: 134 us -> 123 us
    psum x1 -> x0, blocking collectives: 29.5 us -> none  [on_device(): lax.psum(jnp.dot(gained * scale_row[:, None], router_wide, precision=lax....]
    all_gather x0 -> x1, blocking collectives: none -> 17.2 us  [on_device(): lax.all_gather(jnp.dot(gained * scale_row[:, None], router_wide, precisio...]
where the time goes in v1:
time: 261 us; the launch traced here: 260 us
  blocking collectives  123 us (47%)
  waiting for transfers between devices  56.8 us (22%)
  matrix products  36.3 us (14%)
  local copies, waits for them, and re-layouts  21.4 us (8%)
  between operations  14.2 us (5%)
  other arithmetic  4.49 us (2%)
  starting transfers between devices  3.3 us (1%)
    reduce_scatter x1, waiting for transfers between devices, on_device(): lax.psum_scatter(partial_out, 'seq', scatter_dimension=2, tiled=True)  53 us
    all_gather x2, blocking collectives, joined(): pieces = jax.tree.map(lambda part: lax.all_gather(part, axis), value)  42.1 us
    psum x1, blocking collectives, on_device(): total_sq = lax.psum(squares, 'seq')  29.5 us
    all_gather x1, blocking collectives, on_device(): shard_rows = lax.all_gather(dispatched, 'seq', axis=2, tiled=True)  20.2 us
    all_gather x1, blocking collectives, on_device(): lax.all_gather(jnp.dot(gained * scale_row[:, None], router_wide, precisio...  17.2 us
    dynamic_slice x15, local copies, waits for them, and re-layouts, joined(): lax.scan(lambda running, share: (join(running, share), None), head, tail)  13.4 us
    dot_general x1, matrix products, on_device(): jnp.einsum('erf,efd->erd', hidden_act, w_down, preferred_element_type=jnp...  10.9 us
    dot_general x1, matrix products, on_device(): jnp.einsum('ern,enf->erf', shard_rows, w_up, preferred_element_type=jnp.f...  9.94 us
  transfers between devices with their start and end apart: 3, of which 2 were waited for; matrix products, arithmetic and copies ran while one was open for 1% of the time, Pallas kernels for 0%

profile of v1, /device:TPU:0, one launch (start us, length us, event | category | flops | bytes accessed | tf_op | source)
XLA Modules:
  0.0 260.1 jit_solution(2362982785176055378)
XLA Ops:
  6.5 1.6 reshape.56
  8.2 0.9 broadcast_compare_fusion
  9.1 1.8 fusion.48
  10.9 1.4 fusion.4
  12.3 0.7 copy.28
  13.1 23.7 %all-gather = f32[96,4,6]{2,1,0:T(4,128)S(1)} all-gather(f32[6,4,6]{2,1,0:T(4,128)S(1)} %get-tuple-element.74), channel_id=2, replica_groups=mesh['seq'=16,'exp'=2] {'seq'}, dimensions={0}, use_global_device_ids=true | all-gather | bytes 9792 | tf_op jit(solution)/shard_map/all_gather | solution.py:17
  36.8 0.2 fusion.20
  37.0 18.4 %all-gather.1 = f32[96,4,6]{2,1,0:T(4,128)S(1)} all-gather(f32[6,4,6]{2,1,0:T(4,128)S(1)} %fusion.20), channel_id=3, replica_groups=mesh['seq'=16,'exp'=2] {'seq'}, dimensions={0}, use_global_device_ids=true | all-gather | bytes 9792 | tf_op jit(solution)/shard_map/all_gather | solution.py:17
  55.5 0.7 dynamic-slice
  57.0 0.1 fusion.39
  57.1 0.9 slice.32
  58.0 2.3 slice.35
  60.4 16.4 %while.14 = (s32[]{:T(128)}, f32[6,4,6]{2,1,0:T(4,128)S(1)}, f32[6,4,6]{2,1,0:T(4,128)S(1)}, f32[6,4,6,128]{3,2,1,0:T(8,128)S(1)}, f32[15,6,4,6]{3,2,1,0:T(4,128...) while((s32[]{:T(128)}, f32[6,4,6]{2,1,0:T(4,128)S(1)}, ...), condition=%wide.region_3.4_spmd, body=%wide.region_2.3_spmd.sunk | while | flops 56162 | bytes 374501 | solution.py:20
  60.4 0.9 constant_dynamic-slice_fusion.2
  61.3 0.1 fusion.69
  61.5 0.9 constant_dynamic-slice_fusion.2
  62.4 0.1 fusion.69
  62.6 0.9 constant_dynamic-slice_fusion.2
  63.5 0.1 fusion.69
  63.7 0.9 constant_dynamic-slice_fusion.2
  64.6 0.1 fusion.69
  64.8 0.9 constant_dynamic-slice_fusion.2
  65.7 0.1 fusion.69
  65.9 0.9 constant_dynamic-slice_fusion.2
  66.8 0.1 fusion.69
  67.0 0.9 constant_dynamic-slice_fusion.2
  67.9 0.1 fusion.69
  68.0 0.9 constant_dynamic-slice_fusion.2
  68.9 0.1 fusion.69
  69.1 0.9 constant_dynamic-slice_fusion.2
  70.0 0.1 fusion.69
  70.2 0.9 constant_dynamic-slice_fusion.2
  71.1 0.1 fusion.69
  71.3 0.9 constant_dynamic-slice_fusion.2
  72.2 0.1 fusion.69
  72.4 0.9 constant_dynamic-slice_fusion.2
  73.3 0.1 fusion.69
  73.5 0.9 constant_dynamic-slice_fusion.2
  74.4 0.1 fusion.69
  74.6 0.9 constant_dynamic-slice_fusion.2
  75.5 0.1 fusion.69
  75.7 0.9 constant_dynamic-slice_fusion.2
  76.6 0.1 fusion.69
  76.9 0.4 fusion.49
  77.3 8.1 %all-reduce = f32[6,384]{1,0:T(8,128)S(1)} all-reduce(f32[6,384]{1,0:T(8,128)S(1)} %fusion.49), channel_id=6, replica_groups=mesh['seq'=16,'exp'=2] {'exp'}, use_global_device_ids=true, to_apply=%region_4.5.clone | all-reduce | flops 2304 | bytes 18432
  85.4 0.1 multiply_reduce_fusion
  85.5 0.3 select_reduce_fusion
  85.8 29.5 %psum.7 = f32[3]{0:T(128)S(1)} all-reduce(f32[3]{0:T(128)S(1)} %multiply_reduce_fusion), channel_id=1, replica_groups=mesh['seq'=16,'exp'=2] {'seq'}, use_global_device_ids=true, to_apply=%region_9.10 | all-reduce | flops 3 | bytes 24 | tf_op jit(solution)/shard_map/psum | solution.py:85
  115.3 0.2 convolution_bitcast_fusion.2
  115.5 17.2 %all-gather.4 = f32[16,3,8]{2,1,0:T(4,128)S(1)} all-gather(f32[1,3,8]{2,1,0:T(4,128)S(1)} %convolution_bitcast_fusion.2), channel_id=5, replica_groups=mesh['seq'=16,'exp'=2] {'seq'}, dimensions={0}, use_global_device_ids=true | all-gather | bytes 1632 | tf_op jit(solution)/shard_map/all_gather | solution.py:88
  132.7 0.2 fusion.29
  133.0 0.3 fusion.19
  133.2 0.2 convolution_convert_fusion
  133.5 6.3 %all_to_all.36 = bf16[8,3,384]{2,1,0:T(4,128)(2,1)S(1)} all-to-all(bf16[8,3,384]{2,1,0:T(4,128)(2,1)S(1)} %copy.33), channel_id=1, replica_groups=mesh['seq'=16,'exp'=2] {'exp'}, dimensions={0} | all-to-all | bytes 36864 | tf_op jit(solution)/shard_map/all_to_all | solution.py:114
  139.7 20.2 %all_gather.35 = bf16[4,6,6144]{2,1,0:T(8,128)(2,1)S(1)} all-gather(bf16[4,6,384]{2,1,0:T(8,128)(2,1)S(1)} %copy.35), channel_id=1, replica_groups=mesh['seq'=16,'exp'=2] {'seq'}, dimensions={2}, use_global_device_ids=true | all-gather | bytes 313344 | tf_op jit(solution)/shard_map/all_gather | solution.py:115
  159.9 9.9 %fusion.50 = f32[4,6,512]{2,1,0:T(8,128)S(1)} fusion(bf16[4,6,6144]{2,1,0:T(8,128)(2,1)S(1)} %all_gather.35, bf16[4,6144,512]{2,1,0:T(8,128)(2,1)} %param.25), kind=kOutput, calls=%fused_computation.70 | convolution fusion | flops 150994944 | bytes 25509888 | tf_op jit(solution)/shard_map/ern,enf->erf/dot_general | solution.py:116
  169.8 9.9 %fusion.16 = bf16[4,6,512]{2,1,0:T(8,128)(2,1)S(1)} fusion(bf16[4,6,6144]{2,1,0:T(8,128)(2,1)S(1)} %all_gather.35, bf16[4,6144,512]{2,1,0:T(8,128)(2,1)} %param.26, f32[4,6,512]{2,1,0:T(8,128)S(1)} %fusion.50), kind=kOutput, calls=%fused_computation.19 | convolution fusion | flops 151068672 | bytes 25534464 | tf_op jit(solution)/shard_map/ern,enf->erf/dot_general | solution.py:117
  179.7 10.9 %fusion.51 = f32[4,6,6144]{2,1,0:T(8,128)} fusion(bf16[4,6,512]{2,1,0:T(8,128)(2,1)S(1)} %fusion.16, bf16[4,512,6144]{2,1,0:T(8,128)(2,1)} %param.27), kind=kOutput, calls=%fused_computation.71 | convolution fusion | flops 150994944 | bytes 25780224 | tf_op jit(solution)/shard_map/erf,efd->erd/dot_general | solution.py:119
  190.7 53.0 %reduce-scatter.2.cloned.1.call-done = f32[4,6,384]{2,1,0:T(8,128)} async-done(((f32[4,6,6144]{2,1,0:T(8,128)}), f32[4,6,384]{2,1,0:T(8,128)}) %reduce-scatter.2.cloned.1.call-update) | async-done | bytes 36880 | tf_op jit(solution)/shard_map/reduce_scatter | solution.py:123
  243.7 1.4 copy.36
  245.2 3.3 %all-to-all-start.1 = ((f32[4,6,384]{2,0,1:T(4,128)}), f32[4,6,384]{2,0,1:T(4,128)S(1)}, u32[]{:S(2)}, u32[]{:S(2)}) async-start(f32[4,6,384]{2,0,1:T(4,128)} %copy.36), calls=%async_computation.2 | async-start | bytes 73728 | tf_op jit(solution)/shard_map/all_to_all | solution.py:124
  248.4 0.3 convolution_bitcast_fusion.1
  248.7 3.7 %all-to-all-done.1 = f32[4,6,384]{2,0,1:T(4,128)S(1)} async-done(((f32[4,6,384]{2,0,1:T(4,128)}), f32[4,6,384]{2,0,1:T(4,128)S(1)}, u32[]{:S(2)}, u32[]{:S(2)}) %all-to-all-start.1) | async-done | bytes 36896 | tf_op jit(solution)/shard_map/all_to_all | solution.py:124
  252.4 0.8 fusion.18
  (60 shorter events, 1.3 us)
Async XLA Ops:
  6.5 2.5 copy-start
  6.5 50.6 %all-gather.7.cloned.1.call-start = ((), (), s32[]{:S(2)}) async-start(), calls=%async_computation.4 | async-start | bytes 1253376 | tf_op jit(solution)/shard_map/all_gather | solution.py:17
  8.2 2.7 %copy-start.2 = (bf16[6,512,512]{2,1,0:T(8,128)(2,1)S(1)}, bf16[6,512,512]{2,1,0:T(8,128)(2,1)}, u32[]{:S(2)}) copy-start(bf16[6,512,512]{2,1,0:T(8,128)(2,1)} %param.18) | copy-start | bytes 9437188
  10.9 44.5 %copy-start.5 = (s32[3,2]{0,1:T(2,128)S(1)}, s32[3,2]{0,1:T(2,128)}, u32[]{:S(2)}) copy-start(s32[3,2]{0,1:T(2,128)} %param.23) | copy-start | bytes 76
  10.9 44.6 %copy-start.9 = (u32[32]{0:T(128)S(1)}, u32[32]{0:T(128)}, u32[]{:S(2)}) copy-start(u32[32]{0:T(128)} %constant.44) | copy-start | bytes 388
  13.0 230.7 %reduce-scatter.2.cloned.1.call-start = ((), (), s32[]{:S(2)}) async-start(), calls=%async_computation.3 | async-start | bytes 835584 | tf_op jit(solution)/shard_map/reduce_scatter | solution.py:123
  37.0 39.9 %copy-start.3 = (bf16[3072,384]{1,0:T(8,128)(2,1)S(1)}, bf16[3072,384]{1,0:T(8,128)(2,1)}, u32[]{:S(2)}) copy-start(bf16[3072,384]{1,0:T(8,128)(2,1)} %param.20) | copy-start | bytes 7077892
  60.4 25.0 %copy-start.4 = (bf16[3,384]{1,0:T(4,128)(2,1)S(1)}, bf16[3,384]{1,0:T(4,128)(2,1)}, u32[]{:S(2)}) copy-start(bf16[3,384]{1,0:T(4,128)(2,1)} %param.15) | copy-start | bytes 6916
  60.4 25.1 %copy-start.6 = (s32[8]{0:T(128)S(1)}, s32[8]{0:T(128)}, u32[]{:S(2)}) copy-start(s32[8]{0:T(128)} %param.24) | copy-start | bytes 100
  60.4 54.9 %copy-start.7 = (bf16[384,8]{0,1:T(8,128)(2,1)S(1)}, bf16[384,8]{0,1:T(8,128)(2,1)}, u32[]{:S(2)}) copy-start(bf16[384,8]{0,1:T(8,128)(2,1)} %param.22) | copy-start | bytes 18436
  60.4 54.9 %copy-start.8 = (f32[384]{0:T(512)S(1)}, f32[384]{0:T(512)}, u32[]{:S(2)}) copy-start(f32[384]{0:T(512)} %param.21) | copy-start | bytes 4612
  179.7 73.5 %copy-start.1 = (bf16[6,512,512]{2,1,0:T(8,128)(2,1)S(1)}, bf16[6,512,512]{2,1,0:T(8,128)(2,1)}, u32[]{:S(2)}) copy-start(bf16[6,512,512]{2,1,0:T(8,128)(2,1)} %param.17) | copy-start | bytes 9437188
  245.2 7.2 %all-to-all-start.1 = ((f32[4,6,384]{2,0,1:T(4,128)}), f32[4,6,384]{2,0,1:T(4,128)S(1)}, u32[]{:S(2)}, u32[]{:S(2)}) async-start(f32[4,6,384]{2,0,1:T(4,128)} %copy.36), calls=%async_computation.2 | async-start | bytes 73728 | tf_op jit(solution)/shard_map/all_to_all | solution.py:124
Sparse Core Ops, SparseCore 0:
  13.1 41.2 all-gather.6
  190.8 52.8 reduce-scatter.1
